TPU v7x, 32 devices: a whole 2x2x4 slice. The times are simulated.
32 devices in a mesh: grp: 8 (over y, x, core), mem: 4 (over z).
Axes of the slice: x: 2, y: 2, z: 4, core: 2. Of those that a mesh axis runs over, the one named last changes fastest.
Arguments:
- residual: float32 [256, 64, 256], P(('grp', 'mem')), may hold values from -6 to 6
- direction: float32 [256, 64, 256], P(('grp', 'mem')), may hold values from -6 to 6
- local_inverse: bfloat16 [256, 256, 256], P(('grp', 'mem')), may hold values from -1 to 16, as said below
- dirichlet: bfloat16 [256, 256, 256], P(('grp', 'mem')), may hold values from -1 to 16, as said below
- coupling: bfloat16 [256, 24, 256], P(('grp', 'mem')), may hold values from -0.375 to 0.375
- corner_map: int32 [256, 24], P(('grp', 'mem')), may hold values from 0 to 6143
- coarse_factor: bfloat16 [8, 2048, 2048], P('grp'), may hold values from -1 to 3, as said below
Outputs:
- new_residual: float32 [256, 64, 256], P(('grp', 'mem'))
- new_direction: float32 [256, 64, 256], P(('grp', 'mem'))
- step_sizes: float32 [3, 64], replicated
Inputs may be any that keep to these rules, and one draw needn't show every extreme that they name: `local_inverse`: each subdomain's matrix is symmetric positive definite. `dirichlet`: each subdomain's matrix is symmetric positive definite. `coarse_factor`: each group's factor is lower triangular with a positive diagonal.
All inputs are finite; a program needn't handle non-finite values.
Results may differ from a plain program's by a relative error of at most 0.0083.
Values sent between devices are 32-bit elements; how exact they have to be, the bound alone decides.
A program may use at most 128 MiB of HBM per device.

v0:
```python
import jax
import jax.numpy as jnp
from jax import lax
from jax.sharding import PartitionSpec as P

ITERS = 3


highest = lax.Precision.HIGHEST


def from_behind(block, axis, distance):
    devices = range(lax.axis_size(axis))
    route = [((i - distance) % len(devices), i) for i in devices]
    return lax.ppermute(block, axis, route)


def extended(cells, sides, width):
    for axis, dim in sides:
        count = lax.axis_size(axis)
        head = lax.slice_in_dim(cells, 0, width, axis=dim)
        tail = lax.slice_in_dim(cells, cells.shape[dim] - width, cells.shape[dim], axis=dim)
        cells = jnp.concatenate(
            [
                lax.ppermute(tail, axis, [(i, (i + 1) % count) for i in range(count)]),
                cells,
                lax.ppermute(head, axis, [((i + 1) % count, i) for i in range(count)]),
            ],
            axis=dim,
        )
    return cells


def solve_local(matrices, vectors):
    return jnp.einsum(
        "sij,skj->ski", matrices, vectors.astype(jnp.bfloat16), preferred_element_type=jnp.float32
    )


def column_sums(left_side, right_side):
    return jnp.sum(left_side * right_side, axis=(0, 2))


def coarse_solve(factor, coarse_load):
    forward = jax.scipy.linalg.solve_triangular(factor, coarse_load.T, lower=True)
    return jax.scipy.linalg.solve_triangular(factor, forward, lower=True, trans=1).T


def fold_neighbours(partial_value, block_size):
    from_upper = from_behind(partial_value[:, :block_size], "grp", -1)
    from_lower = from_behind(partial_value[:, 2 * block_size :], "grp", 1)
    return partial_value[:, block_size : 2 * block_size] + from_upper + from_lower


def local(residual, direction, local_inverse, dirichlet, coupling, corner_map, coarse_factor):
    sub_count, rhs_count, dofs_count = residual.shape
    corner_count = coupling.shape[1]
    block_size = coarse_factor.shape[1]
    factor = coarse_factor[0].astype(jnp.float32)
    flat_map = corner_map.reshape(-1)
    coupling_wide = coupling.astype(jnp.float32)
    precond = solve_local(dirichlet, residual)
    norm_now = lax.psum(column_sums(residual, precond), ("grp", "mem"))
    step_list = []
    for iteration in range(ITERS):
        solved = solve_local(local_inverse, direction)
        partial_corner = jnp.einsum("ski,sci->skc", solved, coupling_wide, precision=highest)
        flat_corner = partial_corner.transpose(1, 0, 2).reshape(rhs_count, sub_count * corner_count)
        partial_value = (
            jnp.zeros((rhs_count, 3 * block_size), jnp.float32).at[:, flat_map].add(flat_corner)
        )
        folded = fold_neighbours(partial_value, block_size)
        solution = coarse_solve(factor, lax.psum(folded, "mem"))
        widened = extended(solution, (("grp", 1),), block_size)
        picked = widened[:, flat_map].reshape(rhs_count, sub_count, corner_count).transpose(1, 0, 2)
        lifted = jnp.einsum("skc,sci->ski", picked, coupling_wide, precision=highest)
        image = solve_local(local_inverse, direction + lifted)
        curvature = lax.psum(column_sums(direction, image), ("grp", "mem"))
        alpha = norm_now / curvature
        step_list.append(alpha)
        residual = residual - alpha[None, :, None] * image
        precond = solve_local(dirichlet, residual)
        norm_next = lax.psum(column_sums(residual, precond), ("grp", "mem"))
        direction = precond + (norm_next / norm_now)[None, :, None] * direction
        norm_now = norm_next
    return (residual, direction, jnp.stack(step_list))


def solution(mesh):
    return jax.shard_map(
        local,
        mesh=mesh,
        in_specs=(
            P(("grp", "mem"), None, None),
            P(("grp", "mem"), None, None),
            P(("grp", "mem"), None, None),
            P(("grp", "mem"), None, None),
            P(("grp", "mem"), None, None),
            P(("grp", "mem"), None),
            P("grp", None, None),
        ),
        out_specs=(P(("grp", "mem"), None, None), P(("grp", "mem"), None, None), P()),
        check_vma=False,
    )
```

profile of v0, /device:TPU:0, one launch (start us, length us, event | category | flops | bytes accessed | tf_op | source)
XLA Modules:
  0.0 917.8 jit_solution(7679273841835778049)
XLA Ops:
  11.1 3.0 scatter_custom_fusion
  14.1 3.0 fusion.365
  17.2 2.3 copy.30
  21.1 2.9 collective-permute-start
  24.0 11.3 %convert_select_fusion = f32[2048,2048]{1,0:T(8,128)} fusion(bf16[1,2048,2048]{2,1,0:T(8,128)(2,1)} %param.17), kind=kLoop, calls=%fused_computation.8 | loop fusion | flops 12582912 | bytes 25165824 | tf_op jit(solution)/shard_map/jit(_solve_triangular)/triangular_solve | solution.py:46
  37.6 55.7 %while.12 = (s32[]{:T(128)}, f32[2048,2048]{1,0:T(8,128)}, s32[16,2]{0,1:T(2,128)S(1)}, f32[16,128,128]{2,1,0:T(8,128)}, s32[]{:T(128)}) while((s32[]{:T(128)}, f32[2048,2048]{1,0:T(8,128)}, s32[16,2]{0,1:T(2,128)S(1)}, f32[16,128,128]{2,1,0:T(8,128)}, s32[]{:T(128)}) %tuple.417), condition=%wide.while_cond.1, body=%wide.while_body.1.sunk | while | flops 2 | bytes 132205 | solution.py:46
  38.2 2.9 bitcast_dynamic-update-slice_fusion.2
  41.7 2.9 bitcast_dynamic-update-slice_fusion.2
  45.2 2.9 bitcast_dynamic-update-slice_fusion.2
  48.7 2.9 bitcast_dynamic-update-slice_fusion.2
  52.2 2.9 bitcast_dynamic-update-slice_fusion.2
  55.7 2.9 bitcast_dynamic-update-slice_fusion.2
  59.2 2.9 bitcast_dynamic-update-slice_fusion.2
  62.6 2.9 bitcast_dynamic-update-slice_fusion.2
  66.1 2.9 bitcast_dynamic-update-slice_fusion.2
  69.6 2.9 bitcast_dynamic-update-slice_fusion.2
  73.1 2.9 bitcast_dynamic-update-slice_fusion.2
  76.6 2.9 bitcast_dynamic-update-slice_fusion.2
  80.1 2.9 bitcast_dynamic-update-slice_fusion.2
  83.6 2.9 bitcast_dynamic-update-slice_fusion.2
  87.0 2.9 bitcast_dynamic-update-slice_fusion.2
  90.5 2.8 bitcast_dynamic-update-slice_fusion.2
  93.3 158.4 %custom-call.11 = f32[16,128,128]{1,2,0:T(8,128)S(1)} custom-call(f32[16,128,128]{2,1,0:T(8,128)} %get-tuple-element.46), custom_call_target="InvertDiagBlocksLowerTriangular" | custom-call | tf_op jit(solution)/shard_map/jit(_solve_triangular)/triangular_solve | solution.py:46
  287.9 2.2 fusion.23
  308.3 11.7 %collective-permute-done.3 = f32[64,2048]{1,0:T(8,128)S(1)} collective-permute-done((f32[64,2048]{1,0:T(8,128)S(1)}, f32[64,2048]{1,0:T(8,128)S(1)}, u32[]{:S(2)}, u32[]{:S(2)}) %collective-permute-start.3) | collective-permute-done | bytes 524320 | tf_op jit(solution)/shard_map/ppermute | solution.py:27
  322.5 3.2 copy.31
  325.7 2.6 gather_fusion
  329.7 2.4 multiply_reduce_fusion.5
  332.1 39.5 %all-reduce = (f32[64]{0:T(128)S(1)}, f32[64]{0:T(128)S(1)}) all-reduce(f32[64]{0:T(128)S(1)} %fusion.9, f32[64]{0:T(128)S(1)} %get-tuple-element.437), channel_id=1, replica_groups=mesh['grp'=8,'mem'=4] {'grp','mem'}, use_global_device_ids=true, to_apply=%region_1.0 | all-reduce | flops 128 | bytes 1024 | tf_op jit(solution)/shard_map/psum | solution.py:63
  375.1 40.9 %psum.73 = f32[64]{0:T(128)S(1)} all-reduce(f32[64]{0:T(128)S(1)} %get-tuple-element.439), channel_id=1, replica_groups=mesh['grp'=8,'mem'=4] {'grp','mem'}, use_global_device_ids=true, to_apply=%region_7.0 | all-reduce | flops 64 | bytes 512 | tf_op jit(solution)/shard_map/psum | solution.py:83
  419.0 3.0 scatter_custom_fusion.1
  422.0 3.6 fusion.364
  425.6 2.4 copy.33
  427.9 2.4 copy.34
  430.3 2.6 collective-permute-start.4
  432.9 2.3 copy.41
  435.3 8.7 collective-permute-done.5
  444.6 2.2 add_bitcast_fusion.1
  447.3 38.6 %all-reduce.7.cloned.1.call-done = f32[2048,64]{0,1:T(8,128)} async-done(((f32[2048,64]{0,1:T(8,128)}), f32[2048,64]{0,1:T(8,128)}) %all-reduce.7.cloned.1.call-update) | async-done | bytes 524304 | tf_op jit(solution)/shard_map/psum | solution.py:73
  517.6 2.2 fusion.30
  520.8 2.2 fusion.21
  524.0 2.4 fusion.12
  556.5 12.2 %collective-permute-done.7 = f32[64,2048]{1,0:T(8,128)S(1)} collective-permute-done((f32[64,2048]{1,0:T(8,128)S(1)}, f32[64,2048]{1,0:T(8,128)S(1)}, u32[]{:S(2)}, u32[]{:S(2)}) %collective-permute-start.7) | collective-permute-done | bytes 524320 | tf_op jit(solution)/shard_map/ppermute | solution.py:27
  572.0 3.2 copy.35
  575.3 2.6 gather_fusion.1
  579.3 2.4 multiply_reduce_fusion.3
  581.7 39.3 %psum.75 = f32[64]{0:T(128)S(1)} all-reduce(f32[64]{0:T(128)S(1)} %get-tuple-element.479), channel_id=1, replica_groups=mesh['grp'=8,'mem'=4] {'grp','mem'}, use_global_device_ids=true, to_apply=%region_11.0 | all-reduce | flops 64 | bytes 512 | tf_op jit(solution)/shard_map/psum | solution.py:78
  624.5 38.9 %psum.76 = f32[64]{0:T(128)S(1)} all-reduce(f32[64]{0:T(128)S(1)} %get-tuple-element.481), channel_id=1, replica_groups=mesh['grp'=8,'mem'=4] {'grp','mem'}, use_global_device_ids=true, to_apply=%region_13.0 | all-reduce | flops 64 | bytes 512 | tf_op jit(solution)/shard_map/psum | solution.py:83
  666.4 3.0 scatter_custom_fusion.2
  669.4 3.6 fusion.363
  673.0 2.4 copy.37
  675.3 2.3 copy.38
  677.7 2.8 collective-permute-start.8
  680.5 2.4 copy.42
  682.9 7.5 collective-permute-done.9
  692.0 2.2 add_bitcast_fusion
  694.3 39.0 %all-reduce.9.cloned.1.call-done = f32[2048,64]{0,1:T(8,128)} async-done(((f32[2048,64]{0,1:T(8,128)}), f32[2048,64]{0,1:T(8,128)}) %all-reduce.9.cloned.1.call-update) | async-done | bytes 524304 | tf_op jit(solution)/shard_map/psum | solution.py:73
  768.1 2.2 fusion.19
  771.3 2.4 fusion.10
  803.9 12.3 %collective-permute-done.11 = f32[64,2048]{1,0:T(8,128)S(1)} collective-permute-done((f32[64,2048]{1,0:T(8,128)S(1)}, f32[64,2048]{1,0:T(8,128)S(1)}, u32[]{:S(2)}, u32[]{:S(2)}) %collective-permute-start.11) | collective-permute-done | bytes 524320 | tf_op jit(solution)/shard_map/ppermute | solution.py:27
  819.4 3.2 copy.39
  822.6 2.6 gather_fusion.2
  828.3 39.3 %psum.78 = f32[64]{0:T(128)S(1)} all-reduce(f32[64]{0:T(128)S(1)} %get-tuple-element.521), channel_id=1, replica_groups=mesh['grp'=8,'mem'=4] {'grp','mem'}, use_global_device_ids=true, to_apply=%region_17.0 | all-reduce | flops 64 | bytes 512 | tf_op jit(solution)/shard_map/psum | solution.py:78
  869.3 38.9 %psum.79 = f32[64]{0:T(128)S(1)} all-reduce(f32[64]{0:T(128)S(1)} %get-tuple-element.523), channel_id=1, replica_groups=mesh['grp'=8,'mem'=4] {'grp','mem'}, use_global_device_ids=true, to_apply=%region_19.0 | all-reduce | flops 64 | bytes 512 | tf_op jit(solution)/shard_map/psum | solution.py:83
  (636 shorter events, 232.4 us)
Async XLA Ops:
  7.2 1.2 copy-start
  7.2 244.6 %all-reduce.5.cloned.1.call-start = ((), (), s32[]{:S(2)}) async-start(), calls=%async_computation | async-start | bytes 1048576 | tf_op jit(solution)/shard_map/psum | solution.py:73
  19.5 16.1 %collective-permute-start.1 = (f32[64,2048]{1,0:T(8,128)}, f32[64,2048]{1,0:T(8,128)}, u32[]{:S(2)}, u32[]{:S(2)}) collective-permute-start(f32[64,2048]{1,0:T(8,128)} %copy.30), channel_id=1, source_target_pairs={{28,0},{0,4},{4,8},{8,12},{12,16},{16,20},{20,24},{24,28},{29,1},{... | collective-permute-start | bytes 1572872 | tf_op jit(solution)/shard_map/ppermute | solution.py:15
  21.1 14.5 %collective-permute-start = (f32[64,2048]{1,0:T(8,128)}, f32[64,2048]{1,0:T(8,128)S(1)}, u32[]{:S(2)}, u32[]{:S(2)}) collective-permute-start(f32[64,2048]{1,0:T(8,128)} %copy.29), channel_id=1, source_target_pairs={{4,0},{8,4},{12,8},{16,12},{20,16},{24,20},{28,24},{0,28},{5,1},{9... | collective-permute-start | bytes 1572872 | tf_op jit(solution)/shard_map/ppermute | solution.py:15
  37.6 448.3 %all-reduce.7.cloned.1.call-start = ((), (), s32[]{:S(2)}) async-start(), calls=%async_computation.1 | async-start | bytes 1048576 | tf_op jit(solution)/shard_map/psum | solution.py:73
  251.8 39.4 %copy-start.1 = (f32[2048,2048]{1,0:T(8,128)S(1)}, f32[2048,2048]{1,0:T(8,128)}, u32[]{:S(2)}) copy-start(f32[2048,2048]{1,0:T(8,128)} %get-tuple-element.572) | copy-start | bytes 50331652
  272.1 35.6 %copy-start.2 = (bf16[8,256,256]{2,1,0:T(8,128)(2,1)S(1)}, bf16[8,256,256]{2,1,0:T(8,128)(2,1)}, u32[]{:S(2)}) copy-start(bf16[8,256,256]{2,1,0:T(8,128)(2,1)} %param.14) | copy-start | bytes 3145732
  272.1 35.6 %copy-start.9 = (f32[8,64,256]{2,1,0:T(8,128)S(1)}, f32[8,64,256]{2,1,0:T(8,128)}, u32[]{:S(2)}) copy-start(f32[8,64,256]{2,1,0:T(8,128)} %param.11) | copy-start | bytes 1572868
  292.3 35.9 %copy-start.7 = (bf16[8,24,256]{2,1,0:T(8,128)(2,1)S(1)}, bf16[8,24,256]{2,1,0:T(8,128)(2,1)}, u32[]{:S(2)}) copy-start(bf16[8,24,256]{2,1,0:T(8,128)(2,1)} %param.15) | copy-start | bytes 294916
  306.0 13.9 %collective-permute-start.3 = (f32[64,2048]{1,0:T(8,128)S(1)}, f32[64,2048]{1,0:T(8,128)S(1)}, u32[]{:S(2)}, u32[]{:S(2)}) collective-permute-start(f32[64,2048]{1,0:T(8,128)S(1)} %bitcast.583), channel_id=1, source_target_pairs={{4,0},{8,4},{12,8},{16,12},{20,16},{24,20},{28,24},{0,28},{5,1},{9... | collective-permute-start | bytes 1572872 | tf_op jit(solution)/shard_map/ppermute | solution.py:27
  307.7 13.5 %collective-permute-start.2 = (f32[64,2048]{1,0:T(8,128)S(1)}, f32[64,2048]{1,0:T(8,128)S(1)}, u32[]{:S(2)}, u32[]{:S(2)}) collective-permute-start(f32[64,2048]{1,0:T(8,128)S(1)} %bitcast.584), channel_id=1, source_target_pairs={{0,4},{4,8},{8,12},{12,16},{16,20},{20,24},{24,28},{28,0},{1,5},{5... | collective-permute-start | bytes 1572872 | tf_op jit(solution)/shard_map/ppermute | solution.py:25
  373.0 0.8 copy-start.6
  417.4 0.8 copy-start.4
  430.3 13.7 %collective-permute-start.5 = (f32[64,2048]{1,0:T(8,128)}, f32[64,2048]{1,0:T(8,128)}, u32[]{:S(2)}, u32[]{:S(2)}) collective-permute-start(f32[64,2048]{1,0:T(8,128)} %copy.34), channel_id=1, source_target_pairs={{28,0},{0,4},{4,8},{8,12},{12,16},{16,20},{20,24},{24,28},{29,1},{... | collective-permute-start | bytes 1572872 | tf_op jit(solution)/shard_map/ppermute | solution.py:15
  430.3 14.3 %collective-permute-start.4 = (f32[64,2048]{1,0:T(8,128)}, f32[64,2048]{1,0:T(8,128)}, u32[]{:S(2)}, u32[]{:S(2)}) collective-permute-start(f32[64,2048]{1,0:T(8,128)} %copy.33), channel_id=1, source_target_pairs={{4,0},{8,4},{12,8},{16,12},{20,16},{24,20},{28,24},{0,28},{5,1},{9... | collective-permute-start | bytes 1572872 | tf_op jit(solution)/shard_map/ppermute | solution.py:15
  446.9 286.4 %all-reduce.9.cloned.1.call-start = ((), (), s32[]{:S(2)}) async-start(), calls=%async_computation.2 | async-start | bytes 1048576 | tf_op jit(solution)/shard_map/psum | solution.py:73
  555.6 13.2 %collective-permute-start.7 = (f32[64,2048]{1,0:T(8,128)S(1)}, f32[64,2048]{1,0:T(8,128)S(1)}, u32[]{:S(2)}, u32[]{:S(2)}) collective-permute-start(f32[64,2048]{1,0:T(8,128)S(1)} %bitcast.586), channel_id=1, source_target_pairs={{4,0},{8,4},{12,8},{16,12},{20,16},{24,20},{28,24},{0,28},{5,1},{9... | collective-permute-start | bytes 1572872 | tf_op jit(solution)/shard_map/ppermute | solution.py:27
  556.5 14.3 %collective-permute-start.6 = (f32[64,2048]{1,0:T(8,128)S(1)}, f32[64,2048]{1,0:T(8,128)S(1)}, u32[]{:S(2)}, u32[]{:S(2)}) collective-permute-start(f32[64,2048]{1,0:T(8,128)S(1)} %bitcast.587), channel_id=1, source_target_pairs={{0,4},{4,8},{8,12},{12,16},{16,20},{20,24},{24,28},{28,0},{1,5},{5... | collective-permute-start | bytes 1572872 | tf_op jit(solution)/shard_map/ppermute | solution.py:25
  622.4 0.8 copy-start.5
  664.8 0.8 copy-start.3
  677.7 12.7 %collective-permute-start.9 = (f32[64,2048]{1,0:T(8,128)}, f32[64,2048]{1,0:T(8,128)}, u32[]{:S(2)}, u32[]{:S(2)}) collective-permute-start(f32[64,2048]{1,0:T(8,128)} %copy.38), channel_id=1, source_target_pairs={{28,0},{0,4},{4,8},{8,12},{12,16},{16,20},{20,24},{24,28},{29,1},{... | collective-permute-start | bytes 1572872 | tf_op jit(solution)/shard_map/ppermute | solution.py:15
  677.7 14.3 %collective-permute-start.8 = (f32[64,2048]{1,0:T(8,128)}, f32[64,2048]{1,0:T(8,128)}, u32[]{:S(2)}, u32[]{:S(2)}) collective-permute-start(f32[64,2048]{1,0:T(8,128)} %copy.37), channel_id=1, source_target_pairs={{4,0},{8,4},{12,8},{16,12},{20,16},{24,20},{28,24},{0,28},{5,1},{9... | collective-permute-start | bytes 1572872 | tf_op jit(solution)/shard_map/ppermute | solution.py:15
  802.9 13.2 %collective-permute-start.11 = (f32[64,2048]{1,0:T(8,128)S(1)}, f32[64,2048]{1,0:T(8,128)S(1)}, u32[]{:S(2)}, u32[]{:S(2)}) collective-permute-start(f32[64,2048]{1,0:T(8,128)S(1)} %bitcast.580), channel_id=1, source_target_pairs={{4,0},{8,4},{12,8},{16,12},{20,16},{24,20},{28,24},{0,28},{5,1},{9... | collective-permute-start | bytes 1572872 | tf_op jit(solution)/shard_map/ppermute | solution.py:27
  803.9 14.2 %collective-permute-start.10 = (f32[64,2048]{1,0:T(8,128)S(1)}, f32[64,2048]{1,0:T(8,128)S(1)}, u32[]{:S(2)}, u32[]{:S(2)}) collective-permute-start(f32[64,2048]{1,0:T(8,128)S(1)} %bitcast.581), channel_id=1, source_target_pairs={{0,4},{4,8},{8,12},{12,16},{16,20},{20,24},{24,28},{28,0},{1,5},{5... | collective-permute-start | bytes 1572872 | tf_op jit(solution)/shard_map/ppermute | solution.py:25
  868.7 42.0 %copy-start.8 = (f32[8,64,256]{2,1,0:T(8,128)}, f32[8,64,256]{2,1,0:T(8,128)S(1)}, u32[]{:S(2)}) copy-start(f32[8,64,256]{2,1,0:T(8,128)S(1)} %multiply_subtract_fusion) | copy-start | bytes 1572868
Sparse Core Ops, SparseCore 0:
  37.7 39.7 all-reduce.4
  447.0 38.8 all-reduce.6
  694.4 38.8 all-reduce.8
where the time goes:
time: 931 us; the launch traced here: 918 us
  blocking collectives  237 us (25%)
  matrix products  207 us (22%)
  other arithmetic  198 us (21%)
  waiting for transfers between devices  138 us (15%)
  local copies, waits for them, and re-layouts  107 us (11%)
  between operations  18.2 us (2%)
  starting transfers between devices  12.9 us (1%)
    another operation x4, other arithmetic, coarse_solve(): jax.scipy.linalg.solve_triangular(factor, forward, lower=True, trans=1)  170 us
    another operation x93, matrix products, coarse_solve(): jax.scipy.linalg.solve_triangular(factor, coarse_load.T, lower=True)  124 us
    psum x3, blocking collectives, local(): norm_next = lax.psum(column_sums(residual, precond), ('grp', 'mem'))  119 us
    psum x2, blocking collectives, local(): curvature = lax.psum(column_sums(direction, image), ('grp', 'mem'))  78.5 us
    psum x3, waiting for transfers between devices, local(): solution = coarse_solve(factor, lax.psum(folded, 'mem'))  77.6 us
    another operation x93, matrix products, coarse_solve(): jax.scipy.linalg.solve_triangular(factor, forward, lower=True, trans=1)  64.3 us
    another operation x85, local copies, waits for them, and re-layouts, coarse_solve(): jax.scipy.linalg.solve_triangular(factor, forward, lower=True, trans=1)  55.9 us
    psum x1, blocking collectives, local(): norm_now = lax.psum(column_sums(residual, precond), ('grp', 'mem'))  39.5 us
  transfers between devices with their start and end apart: 15, of which 12 were waited for; matrix products, arithmetic and copies ran while one was open for 25% of the time, Pallas kernels for 0%

commit v1 on v0

v1 whole, which is shorter than its diff:
```python
import functools

import jax
import jax.numpy as jnp
from jax import lax
from jax.experimental import pallas as pl
from jax.experimental.pallas import tpu as pltpu
from jax.sharding import PartitionSpec as P

ITERS = 3
TILE = 256
MESH = pl.DeviceIdType.MESH
f32, bf16 = jnp.float32, jnp.bfloat16


def nn(a, b):
    return lax.dot_general(a, b, (((1,), (0,)), ((), ())), preferred_element_type=f32)


def nt(a, b):
    return lax.dot_general(a, b, (((1,), (1,)), ((), ())), preferred_element_type=f32)


def split(x):
    high = x.astype(bf16)
    return high, (x - high.astype(f32)).astype(bf16)


def stacked(x):
    return jnp.concatenate(split(x), axis=0)


def folded(x):
    half = x.shape[0] // 2
    return x[:half] + x[half:]


def invert_blocks(factor_ref, inv_high, inv_low):
    count = factor_ref.shape[0] // TILE
    rows = lax.broadcasted_iota(jnp.int32, (TILE, TILE), 0)
    cols = lax.broadcasted_iota(jnp.int32, (TILE, TILE), 1)

    def one(b, carry):
        at = pl.multiple_of(b * TILE, TILE)
        tile = factor_ref[pl.ds(at, TILE), pl.ds(at, TILE)].astype(f32)
        diagonal = jnp.where(rows == cols, tile, 0.0)
        by_row = 1.0 / jnp.sum(diagonal, axis=1, keepdims=True)
        x = jnp.where(rows == cols, by_row, 0.0)
        size = 1
        while size < TILE:
            below = (rows // size == cols // size + 1) & ((rows // size) % 2 == 1)
            c = jnp.where(below, tile, 0.0).astype(bf16)
            xh, xl = split(x)
            t = nn(c, xh) + nn(c, xl)
            th, tl = split(t)
            x = x - (nn(xh, th) + (nn(xh, tl) + nn(xl, th)))
            size *= 2
        xh, xl = split(x)
        inv_high[b] = xh
        inv_low[b] = xl
        return carry

    lax.fori_loop(0, count, one, 0)


def coarse_solve(loads, factor_ref, inv_high, inv_low):
    count = len(loads)

    def part(i, j):
        return factor_ref[i * TILE : (i + 1) * TILE, j * TILE : (j + 1) * TILE]

    loads = list(loads)
    for i in range(count):
        b = stacked(loads[i])
        loads[i] = folded(nt(b, inv_high[i]) + nt(b, inv_low[i]))
        x = stacked(loads[i])
        for j in range(i + 1, count):
            loads[j] = loads[j] - folded(nt(x, part(j, i)))
    for i in reversed(range(count)):
        b = stacked(loads[i])
        loads[i] = folded(nn(b, inv_high[i]) + nn(b, inv_low[i]))
        x = stacked(loads[i])
        for j in reversed(range(i)):
            loads[j] = loads[j] - folded(nn(x, part(i, j)))
    return loads


def kernel(
    n_grp, n_mem,
    res_in, dir_in, linv, dirich, cpad, cmap, factor,
    res, direc, steps,
    pre, image, onehot, inv_high, inv_low,
    cm_recv, p_send, p_recv, k_send, k_recv, sums, norm,
    cm_s, cm_r, p_s, p_r, k_s, k_r, a_s, a_r,
):
    subs, rhs, dofs = res_in.shape
    wide = cpad.shape[1]
    coarse = factor.shape[0]
    lanes = sums.shape[3]
    total = n_grp * n_mem
    slots = 3 * n_mem
    grp, mem = lax.axis_index("grp"), lax.axis_index("mem")
    me = grp * n_mem + mem
    mine = n_mem + mem
    eye = lax.broadcasted_iota(jnp.int32, (rhs, lanes), 0) == lax.broadcasted_iota(jnp.int32, (rhs, lanes), 1)

    def to_row(column):
        return jnp.sum(jnp.where(eye, column, 0.0), axis=0, keepdims=True)

    def to_column(row):
        return jnp.sum(jnp.where(eye, row, 0.0), axis=1, keepdims=True)

    def wait_bytes(ref, *sems):
        for sem in sems:
            pltpu.make_async_copy(ref, ref, sem).wait()

    def to_owners(source, target, send_sem, recv_sem):
        def one(d, carry):
            slot = (mine + d) % slots
            shift, other = slot // n_mem, slot % n_mem
            pltpu.make_async_remote_copy(
                src_ref=source(other), dst_ref=target(shift * n_mem + mem),
                send_sem=send_sem, recv_sem=recv_sem,
                device_id=((grp + shift + n_grp - 1) % n_grp, other), device_id_type=MESH,
            ).start()
            return carry

        lax.fori_loop(1, slots, one, 0)

    def to_users(source, target, send_sem, recv_sem):
        def one(d, carry):
            slot = (mine + d) % slots
            shift, other = slot // n_mem, slot % n_mem
            pltpu.make_async_remote_copy(
                src_ref=source(slot), dst_ref=target(shift * n_mem + mem),
                send_sem=send_sem, recv_sem=recv_sem,
                device_id=((grp + n_grp + 1 - shift) % n_grp, other), device_id_type=MESH,
            ).start()
            return carry

        lax.fori_loop(1, slots, one, 0)

    def sum_start(r, column):
        sums[r, me] = to_row(column)

        def one(d, carry):
            to = (me + d) % total
            pltpu.make_async_remote_copy(
                src_ref=sums.at[r, me], dst_ref=sums.at[r, me],
                send_sem=a_s.at[r], recv_sem=a_r.at[r],
                device_id=(to // n_mem, to % n_mem), device_id_type=MESH,
            ).start()
            return carry

        lax.fori_loop(1, total, one, 0)

    def sum_finish(r):
        wait_bytes(sums.at[r, pl.ds(0, total - 1)], a_s.at[r], a_r.at[r])
        return jnp.sum(sums[r], axis=0)

    def precondition():
        acc = jnp.zeros((rhs, dofs), f32)
        for s in range(subs):
            value = res[s]
            out = nn(value.astype(bf16), dirich[s])
            pre[s] = out
            acc = acc + value * out
        return jnp.sum(acc, axis=1, keepdims=True)

    to_owners(lambda other: cmap, lambda slot: cm_recv.at[slot], cm_s.at[0], cm_r.at[0])
    cm_recv[mine] = cmap[...]
    res[...] = res_in[...]
    direc[...] = dir_in[...]
    sum_start(0, precondition())
    invert_blocks(factor, inv_high, inv_low)
    wait_bytes(cm_recv.at[pl.ds(0, slots - 1)], cm_s.at[0], cm_r.at[0])
    held = onehot.shape[0] == coarse
    place = lax.broadcasted_iota(jnp.int32, (TILE, wide), 0)

    def fill(start, at):
        for slot in range(slots):
            row = cm_recv[slot] - coarse * (slot // n_mem) - start
            onehot[pl.ds(at, TILE), slot * wide : (slot + 1) * wide] = jnp.where(place == row, 1.0, 0.0).astype(bf16)

    def rows_of(i):
        if held:
            return onehot[i * TILE : (i + 1) * TILE, :]
        fill(i * TILE, 0)
        return onehot[...]

    if held:
        def fill_one(i, carry):
            at = pl.multiple_of(i * TILE, TILE)
            fill(at, at)
            return carry

        lax.fori_loop(0, coarse // TILE, fill_one, 0)
    norm[...] = sum_finish(0)

    def iteration(t, carry):
        partial = jnp.zeros((2 * rhs, wide), f32)
        for s in range(subs):
            solved = nn(direc[s].astype(bf16), linv[s])
            partial = partial + nt(stacked(solved), cpad[s])
        p_send[t] = folded(partial).reshape(p_send.shape[1:])
        to_owners(lambda other: p_send.at[t, other], lambda slot: p_recv.at[t, slot], p_s.at[t], p_r.at[t])
        p_recv[t, mine] = p_send[t, mem]
        wait_bytes(p_recv.at[t, pl.ds(0, slots - 1)], p_s.at[t], p_r.at[t])
        packed = jnp.concatenate([stacked(p_recv[t, slot]) for slot in range(slots)], axis=1)
        loads = [folded(nt(packed, rows_of(i))) for i in range(coarse // TILE)]
        loads = coarse_solve(loads, factor, inv_high, inv_low)
        if held:
            packed = jnp.concatenate([stacked(x) for x in loads], axis=1)
            for slot in range(slots):
                k_send[t, slot] = folded(nn(packed, onehot[:, slot * wide : (slot + 1) * wide]))
        else:
            wanted = sum(folded(nn(stacked(x), rows_of(i))) for i, x in enumerate(loads))
            for slot in range(slots):
                k_send[t, slot] = wanted[:, slot * wide : (slot + 1) * wide]
        to_users(lambda slot: k_send.at[t, slot], lambda slot: k_recv.at[t, slot], k_s.at[t], k_r.at[t])
        k_recv[t, mine] = k_send[t, mine]
        wait_bytes(k_recv.at[t, pl.ds(0, slots - 1)], k_s.at[t], k_r.at[t])
        got = k_recv[t].reshape(3, rhs, wide)
        picked = stacked(got[0] + got[1] + got[2])
        acc = jnp.zeros((rhs, dofs), f32)
        for s in range(subs):
            now = direc[s]
            lifted = folded(nn(picked, cpad[s]))
            out = nn((now + lifted).astype(bf16), linv[s])
            image[s] = out
            acc = acc + now * out
        sum_start(2 * t + 1, jnp.sum(acc, axis=1, keepdims=True))
        norm_now = norm[...]
        curvature = sum_finish(2 * t + 1)
        alpha = norm_now / curvature
        steps[t] = alpha
        column = to_column(alpha)
        for s in range(subs):
            res[s] = res[s] - column * image[s]
        sum_start(2 * t + 2, precondition())
        norm_next = sum_finish(2 * t + 2)
        column = to_column(norm_next / norm_now)
        for s in range(subs):
            direc[s] = pre[s] + column * direc[s]
        norm[...] = norm_next
        return carry

    lax.fori_loop(0, steps.shape[0], iteration, 0)


def local(n_grp, n_mem, residual, direction, local_inverse, dirichlet, coupling, corner_map, coarse_factor):
    subs, rhs, dofs = residual.shape
    corners = coupling.shape[1]
    coarse = coarse_factor.shape[1]
    used = subs * corners
    wide = -(-used // TILE) * TILE
    lanes = -(-rhs // 128) * 128
    total, slots, share = n_grp * n_mem, 3 * n_mem, rhs // n_mem
    own = jnp.arange(wide) // corners
    tiled = jnp.pad(jnp.tile(coupling, (1, subs, 1)), ((0, 0), (0, wide - used), (0, 0)))
    cpad = jnp.where(own[None, :, None] == jnp.arange(subs)[:, None, None], tiled, 0).astype(bf16)
    cmap = jnp.pad(corner_map.reshape(1, used), ((0, 0), (0, wide - used)), constant_values=-1)
    vmem = pl.BlockSpec(memory_space=pltpu.VMEM)
    dma = pltpu.SemaphoreType.DMA
    res, direc, steps = pl.pallas_call(
        functools.partial(kernel, n_grp, n_mem),
        out_shape=(
            jax.ShapeDtypeStruct(residual.shape, f32),
            jax.ShapeDtypeStruct(direction.shape, f32),
            jax.ShapeDtypeStruct((ITERS, 1, lanes), f32),
        ),
        in_specs=[vmem] * 7,
        out_specs=(vmem,) * 3,
        scratch_shapes=[
            pltpu.VMEM((subs, rhs, dofs), f32),
            pltpu.VMEM((subs, rhs, dofs), f32),
            pltpu.VMEM((coarse if slots <= 12 else TILE, slots * wide), bf16),
            pltpu.VMEM((coarse // TILE, TILE, TILE), bf16),
            pltpu.VMEM((coarse // TILE, TILE, TILE), bf16),
            pltpu.VMEM((slots, 1, wide), jnp.int32),
            pltpu.VMEM((ITERS, n_mem, share, wide), f32),
            pltpu.VMEM((ITERS, slots, share, wide), f32),
            pltpu.VMEM((ITERS, slots, share, wide), f32),
            pltpu.VMEM((ITERS, slots, share, wide), f32),
            pltpu.VMEM((2 * ITERS + 1, total, 1, lanes), f32),
            pltpu.VMEM((1, lanes), f32),
            dma((1,)), dma((1,)),
            dma((ITERS,)), dma((ITERS,)), dma((ITERS,)), dma((ITERS,)),
            dma((2 * ITERS + 1,)), dma((2 * ITERS + 1,)),
        ],
        compiler_params=pltpu.CompilerParams(has_side_effects=True, vmem_limit_bytes=62 * 2**20),
    )(residual, direction, local_inverse, dirichlet, cpad, cmap, coarse_factor[0])
    return res, direc, steps[:, 0, :rhs]


def solution(mesh):
    return jax.shard_map(
        functools.partial(local, mesh.shape["grp"], mesh.shape["mem"]),
        mesh=mesh,
        in_specs=(
            P(("grp", "mem"), None, None),
            P(("grp", "mem"), None, None),
            P(("grp", "mem"), None, None),
            P(("grp", "mem"), None, None),
            P(("grp", "mem"), None, None),
            P(("grp", "mem"), None),
            P("grp", None, None),
        ),
        out_specs=(P(("grp", "mem"), None, None), P(("grp", "mem"), None, None), P()),
        check_vma=False,
    )
```

time: 931 us -> 170 us (0.18); the launches traced: 918 us -> 169 us
  blocking collectives: 237 us -> 0 us
  matrix products: 207 us -> 0 us
  other arithmetic: 198 us -> 1.21 us
  Pallas kernels: 0 us -> 160 us
  waiting for transfers between devices: 138 us -> 0 us
  local copies, waits for them, and re-layouts: 107 us -> 7.26 us
  between operations: 18.2 us -> 0.64 us
  starting transfers between devices: 12.9 us -> 0 us
    psum x6 -> x0, blocking collectives: 237 us -> none  [the longest x3 119 us: local(): norm_next = lax.psum(column_sums(residual, precond), ('grp', 'mem'))]
    another operation x186 -> x0, matrix products: 188 us -> none  [the longest x93 124 us: coarse_solve(): jax.scipy.linalg.solve_triangular(factor, coarse_load.T, lower=True)]
    another operation x5 -> x0, other arithmetic: 170 us -> none  [the longest x4 170 us: coarse_solve(): jax.scipy.linalg.solve_triangular(factor, forward, lower=True, trans=1)]
    pallas_call x0 -> x1, Pallas kernels: none -> 160 us  [local(): pl.pallas_call(functools.partial(kernel, n_grp, n_mem), out_shape=(jax.Sh...]
    psum x3 -> x0, waiting for transfers between devices: 77.6 us -> none  [local(): solution = coarse_solve(factor, lax.psum(folded, 'mem'))]
    ppermute x12 -> x0, waiting for transfers between devices: 59.9 us -> none  [the longest x3 36.2 us: extended(): lax.ppermute(head, axis, [((i + 1) % count, i) for i in range(count)])]
    another operation x85 -> x1, local copies, waits for them, and re-layouts: 55.9 us -> 0.94 us  [local(): jnp.tile(coupling, (1, subs, 1))]
    slice x9 -> x0, local copies, waits for them, and re-layouts: 23 us -> none  [the longest x6 16 us: fold_neighbours(): from_upper = from_behind(partial_value[:, :block_size], 'grp', -1)]
  transfers between devices with their start and end apart: 15 -> 0, of which waited for: 12 -> 0; matrix products, arithmetic and copies ran while one was open for 25% -> 0% of each run, Pallas kernels for 0% -> 0%
where the time goes in v1:
time: 170 us; the launch traced here: 169 us
  Pallas kernels  160 us (94%)
  local copies, waits for them, and re-layouts  7.26 us (4%)
    pallas_call x1, Pallas kernels, local(): pl.pallas_call(functools.partial(kernel, n_grp, n_mem), out_shape=(jax.Sh...  160 us
    unnamed x3, local copies, waits for them, and re-layouts  4.98 us

profile of v1, /device:TPU:0, one launch (start us, length us, event | category | flops | bytes accessed | tf_op | source)
XLA Modules:
  0.0 169.2 jit_solution(999612448500137059)
XLA Ops:
  0.6 0.8 reshape.49
  1.4 0.6 pad.9.cmap
  2.0 0.9 tile.4
  2.9 1.2 pad_select_fusion.cpad
  4.1 160.1 %shard_map.94 = (f32[8,64,256]{2,1,0:T(8,128)}, f32[8,64,256]{2,1,0:T(8,128)}, f32[3,1,128]{2,1,0:T(1,128)}) custom-call(f32[8,64,256]{2,1,0:T(8,128)} %res_in.1, f32[8,64,256]{2,1,0:T(8,128)} %dir_in.1, bf16[8,256,256]{2,1,0:T(8,128)(2,1)} %linv.1, bf16[8,256,256]{2,1,0:T(8,128)(2,1)} %dirich.1, bf16[8,256,256]{2,1,0:T(8,128)(2,1)} %pad_select_fusion.cpad, ...), custom_call_target="tpu_custom_call" | custom-call | tf_op jit(solution)/shard_map/pallas_call | solution.py:265
  164.2 1.2 copy.12
  165.5 1.9 %copy.15 = f32[8,64,256]{2,1,0:T(8,128)} copy(f32[8,64,256]{2,1,0:T(8,128)} %get-tuple-element.12) | data formatting | bytes 1048576
  167.3 1.9 %copy.16 = f32[8,64,256]{2,1,0:T(8,128)} copy(f32[8,64,256]{2,1,0:T(8,128)} %get-tuple-element.13) | data formatting | bytes 1048576
  (2 shorter events, 0.0 us)

commit v2 on v1

--- a/solution.py
+++ b/solution.py
@@ -9,6 +9,7 @@
 
 ITERS = 3
 TILE = 256
+GROUP = 4
 MESH = pl.DeviceIdType.MESH
 f32, bf16 = jnp.float32, jnp.bfloat16
 
@@ -37,30 +38,50 @@
 
 def invert_blocks(factor_ref, inv_high, inv_low):
     count = factor_ref.shape[0] // TILE
+    together = GROUP if count % GROUP == 0 else 1
+    half = TILE // 2
     rows = lax.broadcasted_iota(jnp.int32, (TILE, TILE), 0)
     cols = lax.broadcasted_iota(jnp.int32, (TILE, TILE), 1)
 
-    def one(b, carry):
-        at = pl.multiple_of(b * TILE, TILE)
-        tile = factor_ref[pl.ds(at, TILE), pl.ds(at, TILE)].astype(f32)
-        diagonal = jnp.where(rows == cols, tile, 0.0)
-        by_row = 1.0 / jnp.sum(diagonal, axis=1, keepdims=True)
-        x = jnp.where(rows == cols, by_row, 0.0)
-        size = 1
-        while size < TILE:
-            below = (rows // size == cols // size + 1) & ((rows // size) % 2 == 1)
-            c = jnp.where(below, tile, 0.0).astype(bf16)
+    def below(size):
+        return (rows // size == cols // size + 1) & ((rows // size) % 2 == 1)
+
+    def product(x, c):
+        xh, xl = split(x[0])
+        t = nn(c, xh) + nn(c, xl)
+        th, tl = split(t)
+        xh, xl = split(x[1])
+        return nn(xh, th) + (nn(xh, tl) + nn(xl, th))
+
+    def some(step, carry):
+        tiles, found = [], []
+        for k in range(together):
+            at = pl.multiple_of((step * together + k) * TILE, TILE)
+            tile = factor_ref[pl.ds(at, TILE), pl.ds(at, TILE)].astype(f32)
+            diagonal = jnp.where(rows == cols, tile, 0.0)
+            by_row = 1.0 / jnp.sum(diagonal, axis=1, keepdims=True)
+            by_col = 1.0 / jnp.sum(diagonal, axis=0, keepdims=True)
+            first = jnp.where(below(1), -by_row * tile * by_col, 0.0)
+            tiles.append(tile)
+            found.append(jnp.where(rows == cols, by_row, first))
+        size = 2
+        while size < half:
+            mask = below(size)
+            for k in range(together):
+                c = jnp.where(mask, tiles[k], 0.0).astype(bf16)
+                found[k] = found[k] - product((found[k], found[k]), c)
+            size *= 2
+        for k in range(together):
+            x = found[k]
+            upper, lower = x[:half, :half], x[half:, half:]
+            corner = -product((upper, lower), tiles[k][half:, :half].astype(bf16))
+            x = jnp.concatenate([x[:half], jnp.concatenate([corner, lower], axis=1)], axis=0)
             xh, xl = split(x)
-            t = nn(c, xh) + nn(c, xl)
-            th, tl = split(t)
-            x = x - (nn(xh, th) + (nn(xh, tl) + nn(xl, th)))
-            size *= 2
-        xh, xl = split(x)
-        inv_high[b] = xh
-        inv_low[b] = xl
+            inv_high[step * together + k] = xh
+            inv_low[step * together + k] = xl
         return carry
 
-    lax.fori_loop(0, count, one, 0)
+    lax.fori_loop(0, count // together, some, 0)
 
 
 def coarse_solve(loads, factor_ref, inv_high, inv_low):
@@ -87,16 +108,18 @@
 
 def kernel(
     n_grp, n_mem,
-    res_in, dir_in, linv, dirich, cpad, cmap, factor,
+    res_in, dir_in, linv, dirich, cpad, cmap, factor_in,
     res, direc, steps,
-    pre, image, onehot, inv_high, inv_low,
+    pre, image, change, onehot, factor, inv_high, inv_low, load_p, load_d,
     cm_recv, p_send, p_recv, k_send, k_recv, sums, norm,
-    cm_s, cm_r, p_s, p_r, k_s, k_r, a_s, a_r,
+    f_s, cm_s, cm_r, p_s, p_r, k_s, k_r, a_s, a_r,
 ):
     subs, rhs, dofs = res_in.shape
     wide = cpad.shape[1]
     coarse = factor.shape[0]
     lanes = sums.shape[3]
+    share = p_send.shape[2]
+    last = steps.shape[0] - 1
     total = n_grp * n_mem
     slots = 3 * n_mem
     grp, mem = lax.axis_index("grp"), lax.axis_index("mem")
@@ -104,8 +127,15 @@
     mine = n_mem + mem
     eye = lax.broadcasted_iota(jnp.int32, (rhs, lanes), 0) == lax.broadcasted_iota(jnp.int32, (rhs, lanes), 1)
 
+    eye_share = lax.broadcasted_iota(jnp.int32, (share, lanes), 1) == mem * share + lax.broadcasted_iota(
+        jnp.int32, (share, lanes), 0
+    )
+
     def to_row(column):
         return jnp.sum(jnp.where(eye, column, 0.0), axis=0, keepdims=True)
+
+    def to_share(row):
+        return jnp.sum(jnp.where(eye_share, row, 0.0), axis=1, keepdims=True)
 
     def to_column(row):
         return jnp.sum(jnp.where(eye, row, 0.0), axis=1, keepdims=True)
@@ -140,8 +170,10 @@
 
         lax.fori_loop(1, slots, one, 0)
 
-    def sum_start(r, column):
-        sums[r, me] = to_row(column)
+    def sum_start(r, products):
+        columns = [to_row(jnp.sum(x, axis=1, keepdims=True)) for x in products]
+        columns += [jnp.zeros((1, lanes), f32)] * (4 - len(columns))
+        sums[r, me] = jnp.concatenate(columns, axis=0)
 
         def one(d, carry):
             to = (me + d) % total
@@ -158,20 +190,37 @@
         wait_bytes(sums.at[r, pl.ds(0, total - 1)], a_s.at[r], a_r.at[r])
         return jnp.sum(sums[r], axis=0)
 
-    def precondition():
-        acc = jnp.zeros((rhs, dofs), f32)
+    def partial_of(values):
+        acc = jnp.zeros((2 * rhs, wide), f32)
         for s in range(subs):
-            value = res[s]
-            out = nn(value.astype(bf16), dirich[s])
-            pre[s] = out
-            acc = acc + value * out
-        return jnp.sum(acc, axis=1, keepdims=True)
-
+            solved = folded(nn(stacked(values[s]), linv[s]))
+            acc = acc + nt(stacked(solved), cpad[s])
+        return folded(acc)
+
+    def partial_start(r, values):
+        p_send[r] = partial_of(values).reshape(p_send.shape[1:])
+        to_owners(lambda other: p_send.at[r, other], lambda slot: p_recv.at[r, slot], p_s.at[r], p_r.at[r])
+        p_recv[r, mine] = p_send[r, mem]
+
+    def partial_finish(r):
+        wait_bytes(p_recv.at[r, pl.ds(0, slots - 1)], p_s.at[r], p_r.at[r])
+
+    factor_copy = pltpu.make_async_copy(factor_in, factor, f_s.at[0])
+    factor_copy.start()
     to_owners(lambda other: cmap, lambda slot: cm_recv.at[slot], cm_s.at[0], cm_r.at[0])
     cm_recv[mine] = cmap[...]
-    res[...] = res_in[...]
-    direc[...] = dir_in[...]
-    sum_start(0, precondition())
+    acc = jnp.zeros((rhs, dofs), f32)
+    for s in range(subs):
+        value = res_in[s]
+        out = folded(nn(stacked(value), dirich[s]))
+        res[s] = value
+        direc[s] = dir_in[s]
+        pre[s] = out
+        acc = acc + value * out
+    sum_start(0, [acc])
+    partial_start(0, direc)
+    partial_start(1, pre)
+    factor_copy.wait()
     invert_blocks(factor, inv_high, inv_low)
     wait_bytes(cm_recv.at[pl.ds(0, slots - 1)], cm_s.at[0], cm_r.at[0])
     held = onehot.shape[0] == coarse
@@ -195,19 +244,23 @@
             return carry
 
         lax.fori_loop(0, coarse // TILE, fill_one, 0)
-    norm[...] = sum_finish(0)
+    def scattered(rounds):
+        packed = jnp.concatenate(
+            [jnp.concatenate([stacked(p_recv[r, slot]) for slot in range(slots)], axis=1) for r in rounds], axis=0
+        )
+        for i in range(coarse // TILE):
+            out = nt(packed, rows_of(i))
+            yield i * TILE, [folded(out[2 * share * k : 2 * share * (k + 1)]) for k in range(len(rounds))]
+
+    partial_finish(0)
+    partial_finish(1)
+    for at, (first, second) in scattered((0, 1)):
+        load_d[:, at : at + TILE] = first
+        load_p[:, at : at + TILE] = second
+    norm[...] = sum_finish(0)[0:1]
 
     def iteration(t, carry):
-        partial = jnp.zeros((2 * rhs, wide), f32)
-        for s in range(subs):
-            solved = nn(direc[s].astype(bf16), linv[s])
-            partial = partial + nt(stacked(solved), cpad[s])
-        p_send[t] = folded(partial).reshape(p_send.shape[1:])
-        to_owners(lambda other: p_send.at[t, other], lambda slot: p_recv.at[t, slot], p_s.at[t], p_r.at[t])
-        p_recv[t, mine] = p_send[t, mem]
-        wait_bytes(p_recv.at[t, pl.ds(0, slots - 1)], p_s.at[t], p_r.at[t])
-        packed = jnp.concatenate([stacked(p_recv[t, slot]) for slot in range(slots)], axis=1)
-        loads = [folded(nt(packed, rows_of(i))) for i in range(coarse // TILE)]
+        loads = [load_d[:, at : at + TILE] for at in range(0, coarse, TILE)]
         loads = coarse_solve(loads, factor, inv_high, inv_low)
         if held:
             packed = jnp.concatenate([stacked(x) for x in loads], axis=1)
@@ -222,30 +275,50 @@
         wait_bytes(k_recv.at[t, pl.ds(0, slots - 1)], k_s.at[t], k_r.at[t])
         got = k_recv[t].reshape(3, rhs, wide)
         picked = stacked(got[0] + got[1] + got[2])
-        acc = jnp.zeros((rhs, dofs), f32)
+        zero = jnp.zeros((rhs, dofs), f32)
+        curve, cross, square = zero, zero, zero
         for s in range(subs):
             now = direc[s]
             lifted = folded(nn(picked, cpad[s]))
             out = nn((now + lifted).astype(bf16), linv[s])
             image[s] = out
-            acc = acc + now * out
-        sum_start(2 * t + 1, jnp.sum(acc, axis=1, keepdims=True))
+            curve = curve + now * out
+            moved = folded(nn(stacked(out), dirich[s]))
+            change[s] = moved
+            cross = cross + out * pre[s]
+            square = square + out * moved
+        sum_start(t + 1, [curve, cross, square])
+
+        @pl.when(t < last)
+        def _():
+            partial_start(t + 2, change)
+
         norm_now = norm[...]
-        curvature = sum_finish(2 * t + 1)
-        alpha = norm_now / curvature
+        summed = sum_finish(t + 1)
+        alpha = norm_now / summed[0:1]
+        norm_next = norm_now - alpha * (2.0 * summed[1:2] - alpha * summed[2:3])
+        beta = norm_next / norm_now
         steps[t] = alpha
-        column = to_column(alpha)
+        norm[...] = norm_next
+        by_alpha, by_beta = to_column(alpha), to_column(beta)
         for s in range(subs):
-            res[s] = res[s] - column * image[s]
-        sum_start(2 * t + 2, precondition())
-        norm_next = sum_finish(2 * t + 2)
-        column = to_column(norm_next / norm_now)
-        for s in range(subs):
-            direc[s] = pre[s] + column * direc[s]
-        norm[...] = norm_next
+            res[s] = res[s] - by_alpha * image[s]
+            new = pre[s] - by_alpha * change[s]
+            pre[s] = new
+            direc[s] = new + by_beta * direc[s]
+
+        @pl.when(t < last)
+        def _():
+            share_alpha, share_beta = to_share(alpha), to_share(beta)
+            partial_finish(t + 2)
+            for at, (moved,) in scattered((t + 2,)):
+                new = load_p[:, at : at + TILE] - share_alpha * moved
+                load_p[:, at : at + TILE] = new
+                load_d[:, at : at + TILE] = new + share_beta * load_d[:, at : at + TILE]
+
         return carry
 
-    lax.fori_loop(0, steps.shape[0], iteration, 0)
+    lax.fori_loop(0, last + 1, iteration, 0)
 
 
 def local(n_grp, n_mem, residual, direction, local_inverse, dirichlet, coupling, corner_map, coarse_factor):
@@ -269,24 +342,28 @@
             jax.ShapeDtypeStruct(direction.shape, f32),
             jax.ShapeDtypeStruct((ITERS, 1, lanes), f32),
         ),
-        in_specs=[vmem] * 7,
+        in_specs=[vmem] * 6 + [pl.BlockSpec(memory_space=pl.ANY)],
         out_specs=(vmem,) * 3,
         scratch_shapes=[
             pltpu.VMEM((subs, rhs, dofs), f32),
             pltpu.VMEM((subs, rhs, dofs), f32),
+            pltpu.VMEM((subs, rhs, dofs), f32),
             pltpu.VMEM((coarse if slots <= 12 else TILE, slots * wide), bf16),
+            pltpu.VMEM((coarse, coarse), bf16),
             pltpu.VMEM((coarse // TILE, TILE, TILE), bf16),
             pltpu.VMEM((coarse // TILE, TILE, TILE), bf16),
+            pltpu.VMEM((share, coarse), f32),
+            pltpu.VMEM((share, coarse), f32),
             pltpu.VMEM((slots, 1, wide), jnp.int32),
-            pltpu.VMEM((ITERS, n_mem, share, wide), f32),
+            pltpu.VMEM((ITERS + 1, n_mem, share, wide), f32),
+            pltpu.VMEM((ITERS + 1, slots, share, wide), f32),
             pltpu.VMEM((ITERS, slots, share, wide), f32),
             pltpu.VMEM((ITERS, slots, share, wide), f32),
-            pltpu.VMEM((ITERS, slots, share, wide), f32),
-            pltpu.VMEM((2 * ITERS + 1, total, 1, lanes), f32),
+            pltpu.VMEM((ITERS + 1, total, 4, lanes), f32),
             pltpu.VMEM((1, lanes), f32),
-            dma((1,)), dma((1,)),
-            dma((ITERS,)), dma((ITERS,)), dma((ITERS,)), dma((ITERS,)),
-            dma((2 * ITERS + 1,)), dma((2 * ITERS + 1,)),
+            dma((1,)), dma((1,)), dma((1,)),
+            dma((ITERS + 1,)), dma((ITERS + 1,)), dma((ITERS,)), dma((ITERS,)),
+            dma((ITERS + 1,)), dma((ITERS + 1,)),
         ],
         compiler_params=pltpu.CompilerParams(has_side_effects=True, vmem_limit_bytes=62 * 2**20),
     )(residual, direction, local_inverse, dirichlet, cpad, cmap, coarse_factor[0])

time: 170 us -> 120 us (0.71)
  Pallas kernels: 160 us -> 110 us
    pallas_call x1, Pallas kernels: 160 us -> 110 us  [local(): pl.pallas_call(functools.partial(kernel, n_grp, n_mem), out_shape=(jax.Sh...]
where the time goes in v2:
time: 120 us
  Pallas kernels  110 us (92%)
  local copies, waits for them, and re-layouts  7.26 us (6%)
  other arithmetic  1.21 us (1%)
    pallas_call x1, Pallas kernels, local(): pl.pallas_call(functools.partial(kernel, n_grp, n_mem), out_shape=(jax.Sh...  110 us
    unnamed x3, local copies, waits for them, and re-layouts  4.98 us

profile of v2, /device:TPU:0, one launch (start us, length us, event | category | flops | bytes accessed | tf_op | source)
XLA Modules:
  0.0 119.6 jit_solution(12340020474555644069)
XLA Ops:
  0.6 0.8 reshape.49
  1.4 0.6 pad.9.cmap
  2.0 0.9 tile.4
  2.9 1.2 pad_select_fusion.cpad
  4.1 110.5 %shard_map.94 = (f32[8,64,256]{2,1,0:T(8,128)}, f32[8,64,256]{2,1,0:T(8,128)}, f32[3,1,128]{2,1,0:T(1,128)}) custom-call(f32[8,64,256]{2,1,0:T(8,128)} %res_in.1, f32[8,64,256]{2,1,0:T(8,128)} %dir_in.1, bf16[8,256,256]{2,1,0:T(8,128)(2,1)} %linv.1, bf16[8,256,256]{2,1,0:T(8,128)(2,1)} %dirich.1, bf16[8,256,256]{2,1,0:T(8,128)(2,1)} %pad_select_fusion.cpad, ...), custom_call_target="tpu_custom_call" | custom-call | tf_op jit(solution)/shard_map/pallas_call | solution.py:338
  114.6 1.2 %copy.12 = f32[3,1,64]{2,0,1:T(4,128)} copy(f32[3,1,64]{2,1,0:T(1,128)} %bitcast.9) | data formatting | bytes 1536
  115.9 1.9 %copy.15 = f32[8,64,256]{2,1,0:T(8,128)} copy(f32[8,64,256]{2,1,0:T(8,128)} %get-tuple-element.12) | data formatting | bytes 1048576
  117.7 1.9 %copy.16 = f32[8,64,256]{2,1,0:T(8,128)} copy(f32[8,64,256]{2,1,0:T(8,128)} %get-tuple-element.13) | data formatting | bytes 1048576
  (2 shorter events, 0.0 us)
